TPU v7x, 256 devices: a whole 4x4x8 slice. The times are simulated.
256 devices in a mesh: dp: 16 (over y, x), sp: 8 (over z), shift: 2 (over core).
Axes of the slice: x: 4, y: 4, z: 8, core: 2. Of those that a mesh axis runs over, the one named last changes fastest.
Arguments:
- query_rows: bfloat16 [32, 2048, 32, 128], P(('shift', 'dp'), 'sp'), parts along dimension 0, may hold values from -6 to 6
- key_rows: bfloat16 [32, 2048, 32, 128], P(('shift', 'dp'), 'sp'), parts along dimension 0, may hold values from -6 to 6
- value_rows: bfloat16 [32, 2048, 32, 128], P(('shift', 'dp'), 'sp'), parts along dimension 0, may hold values from -6 to 6
- out_weight: bfloat16 [8192, 4096], P(('shift', 'dp')), parts along dimension 0, may hold values from -0.09375 to 0.09375
Outputs:
- mixer_out: bfloat16 [32, 2048, 4096], P(('shift', 'dp'), 'sp'), parts along dimension 0
There are 2 independent parts, one for each index of `shift`. A program takes and returns all parts, laid end to end along the dimension named above; each array names one. Nothing has to cross between parts.
All inputs are finite; a program needn't handle non-finite values.
Results may differ from a plain program's by a relative error of at most 0.006.
Values may be sent and summed in bfloat16 or wider, within the bound.
A program may use at most 128 MiB of HBM per device.

v0:
```python
import jax
import jax.numpy as jnp
from jax import lax
from jax.sharding import PartitionSpec as P


def feature_map(values):
    wide = values.astype(jnp.float32)
    return jnp.where(wide > 0.0, wide + 1.0, jnp.exp(jnp.minimum(wide, 0.0))).astype(jnp.bfloat16)


def finish_heads(read, count):
    result = read * count**0.5
    return result.astype(jnp.bfloat16)


def ask_state(features, state, mass):
    top = jnp.einsum(
        "bthd,bhde->bthe", features, state.astype(jnp.bfloat16), preferred_element_type=jnp.float32
    )
    bottom = jnp.einsum(
        "bthd,bhd->bth", features.astype(jnp.float32), mass, precision=lax.Precision.HIGHEST
    )
    return top / (bottom + 0.001)[..., None]


def body(query_rows, key_rows, value_rows, out_weight):
    query_feature, key_feature = (feature_map(query_rows), feature_map(key_rows))
    count = query_rows.shape[1] * lax.axis_size("sp")
    part_state = jnp.einsum(
        "bthd,bthe->bhde", key_feature, value_rows, preferred_element_type=jnp.float32
    )
    part_mass = jnp.sum(key_feature.astype(jnp.float32), axis=1)
    state, mass = lax.psum((part_state, part_mass), "sp")
    read = ask_state(query_feature, state / count, mass / count)
    mixed = finish_heads(read, count)
    mixed = mixed.reshape(mixed.shape[0], mixed.shape[1], -1)
    return jnp.einsum(
        "btw,wv->btv",
        mixed,
        lax.all_gather(out_weight, "dp", axis=0, tiled=True),
        preferred_element_type=jnp.float32,
    ).astype(jnp.bfloat16)


def solution(mesh):
    placed = (
        P(("shift", "dp"), "sp", None, None),
        P(("shift", "dp"), "sp", None, None),
        P(("shift", "dp"), "sp", None, None),
        P(("shift", "dp"), None),
    )
    return jax.shard_map(
        body, mesh=mesh, in_specs=placed, out_specs=P(("shift", "dp"), "sp", None), check_vma=False
    )
```

profile of v0, /device:TPU:1, one launch (start us, length us, event | category | flops | bytes accessed | tf_op | source)
XLA Modules:
  0.0 245.8 jit_solution(8136283110599534945)
XLA Ops:
  7.4 0.0 copy-start
  7.4 0.0 all-reduce.2.cloned.1.call-start
  7.4 3.0 %fusion.21 = (bf16[256,32,128]{2,1,0:T(8,128)(2,1)S(1)}, f32[32,128]{1,0:T(8,128)S(1)}) fusion(bf16[1,256,32,128]{3,2,1,0:T(8,128)(2,1)} %param.5), kind=kLoop, calls=%fused_computation.26 | loop fusion | flops 8384512 | bytes 4210688 | tf_op jit(solution)/shard_map/reshape
  10.3 0.0 copy-done
  10.3 3.0 %fusion.13 = f32[1,32,128,128]{3,2,1,0:T(8,128)} fusion(bf16[256,32,128]{2,1,0:T(8,128)(2,1)S(1)} %bitcast.41, bf16[256,32,128]{2,1,0:T(8,128)(2,1)S(1)} %get-tuple-element.5), kind=kOutput, calls=%fused_computation.23 | convolution fusion | flops 268435456 | bytes 6291456 | tf_op jit(solution)/shard_map/bthd,bthe->bhde/dot_general | solution.py:30
  13.4 0.0 all-reduce.2.cloned.1.call-update
  13.4 0.0 all-gather.2.cloned.1.call-start
  13.4 0.5 all-gather.2.cloned.1.call-update
  14.0 4.0 %fusion.9 = bf16[256,32,128]{2,1,0:T(8,128)(2,1)} fusion(bf16[1,256,32,128]{3,2,1,0:T(8,128)(2,1)} %param.4), kind=kLoop, calls=%fused_computation.18 | loop fusion | flops 6291456 | bytes 4194304 | tf_op jit(solution)/shard_map/reshape.5
  18.0 4.3 %copy.11 = bf16[256,32,128]{0,2,1:T(8,128)(2,1)} copy(bf16[256,32,128]{2,1,0:T(8,128)(2,1)} %fusion.9) | data formatting | bytes 4194304 | tf_op jit(solution)/shard_map/reshape.5
  22.3 29.3 %psum.15 = f32[1,32,128]{2,1,0:T(8,128)S(1)} all-reduce(f32[1,32,128]{2,1,0:T(8,128)S(1)} %bitcast.43), channel_id=1, replica_groups=mesh['dp'=16,'sp'=8,'shift'=2] {'sp'}, use_global_device_ids=true, to_apply=%region_2.3 | all-reduce | flops 4096 | bytes 32768 | tf_op jit(solution)/shard_map/psum | solution.py:34
  51.6 2.5 %fusion.24 = f32[32,1,256]{2,1,0:T(1,128)S(1)} fusion(f32[32,128,1]{1,2,0:T(1,128)S(1)} %bitcast.44, bf16[256,32,128]{0,2,1:T(8,128)(2,1)} %copy.11), kind=kOutput, calls=%fused_computation.31 | convolution fusion | flops 12582912 | bytes 2146304 | tf_op jit(solution)/shard_map/bthd,bhd->bth/dot_general | solution.py:21
  54.1 41.6 %all-reduce.2.cloned.1.call-done = f32[1,32,128,128]{3,2,1,0:T(8,128)} async-done(((f32[1,32,128,128]{3,2,1,0:T(8,128)}), f32[1,32,128,128]{3,2,1,0:T(8,128)}) %all-reduce.2.cloned.1.call-update) | async-done | bytes 2097168 | tf_op jit(solution)/shard_map/psum | solution.py:34
  95.7 4.3 %fusion.8 = bf16[1,256,32,128]{1,3,2,0:T(8,128)(2,1)} fusion(bf16[256,32,128]{0,2,1:T(8,128)(2,1)} %copy.11, f32[256,32]{0,1:T(8,128)S(1)} %fusion.22, f32[1,32,128,128]{3,2,1,0:T(8,128)} %all-reduce.2.cloned.1.call-done), kind=kOutput, calls=%fused_computation.16 | convolution fusion | flops 272629760 | bytes 6324224 | tf_op jit(solution)/shard_map/bthd,bhde->bthe/dot_general | solution.py:18
  100.0 121.8 %all-gather.2.cloned.1.call-done = bf16[4096,4096]{1,0:T(8,128)(2,1)} async-done(((bf16[256,4096]{1,0:T(8,128)(2,1)}), bf16[4096,4096]{1,0:T(8,128)(2,1)}) %all-gather.2.cloned.1.call-update) | async-done | bytes 33554448 | tf_op jit(solution)/shard_map/all_gather | solution.py:41
  221.8 16.6 %fusion = bf16[1,256,4096]{2,1,0:T(8,128)(2,1)} fusion(bf16[256,4096]{0,1:T(8,128)(2,1)} %bitcast.42, bf16[4096,4096]{1,0:T(8,128)(2,1)} %all-gather.2.cloned.1.call-done), kind=kOutput, calls=%fused_computation.7 | convolution fusion | flops 8590983168 | bytes 37748736 | tf_op jit(solution)/shard_map/btw,wv->btv/dot_general | solution.py:38
  (2 shorter events, 0.0 us)
Async XLA Ops:
  7.4 3.0 %copy-start = (bf16[1,256,32,128]{3,2,1,0:T(8,128)(2,1)S(1)}, bf16[1,256,32,128]{3,2,1,0:T(8,128)(2,1)}, u32[]{:S(2)}) copy-start(bf16[1,256,32,128]{3,2,1,0:T(8,128)(2,1)} %param.6) | copy-start | bytes 6291460
  7.4 88.3 %all-reduce.2.cloned.1.call-start = ((), (), s32[]{:S(2)}) async-start(), calls=%async_computation | async-start | bytes 4194304 | tf_op jit(solution)/shard_map/psum | solution.py:34
  13.4 208.4 %all-gather.2.cloned.1.call-start = ((), (), s32[]{:S(2)}) async-start(), calls=%async_computation.1 | async-start | bytes 35651584 | tf_op jit(solution)/shard_map/all_gather | solution.py:41
Sparse Core Ops, SparseCore 0:
  13.5 82.1 all-reduce.1
Sparse Core Ops, SparseCore 1:
  16.3 205.4 all-gather.1
where the time goes:
time: 246 us
  waiting for transfers between devices  164 us (67%)
  blocking collectives  29.3 us (12%)
  matrix products  26.4 us (11%)
  between operations  14.9 us (6%)
  other arithmetic  6.97 us (3%)
  local copies, waits for them, and re-layouts  4.31 us (2%)
    all_gather x1, waiting for transfers between devices, body(): lax.all_gather(out_weight, 'dp', axis=0, tiled=True)  122 us
    psum x1, waiting for transfers between devices, body(): state, mass = lax.psum((part_state, part_mass), 'sp')  41.6 us
    psum x1, blocking collectives, body(): state, mass = lax.psum((part_state, part_mass), 'sp')  29.3 us
    dot_general x1, matrix products, body(): jnp.einsum('btw,wv->btv', mixed, lax.all_gather(out_weight, 'dp', axis=0,...  16.6 us
  transfers between devices with their start and end apart: 2, of which 2 were waited for; matrix products, arithmetic and copies ran while one was open for 6% of the time, Pallas kernels for 0%

commit v1 on v0

--- a/solution.py
+++ b/solution.py
@@ -2,6 +2,25 @@
 import jax.numpy as jnp
 from jax import lax
 from jax.sharding import PartitionSpec as P
+from jax.lax import axis_index, axis_size, ppermute
+
+
+def _draft_counts(message, pos_dim, panel):
+    tile_out = axis_size("dp")
+    y2, outcome_arr, big = (tile_out, axis_index("dp"), message.shape[pos_dim])
+    pieces_in = tuple(((no, (no + 1) % y2) for no in range(y2)))
+    so_far_all = tuple(((no, (no - 1) % y2) for no in range(y2)))
+    w1 = y2 // 2
+    found_now = x_new = message
+    built = panel(message, outcome_arr * big)
+    for s in range(1, w1 + 1):
+        found_now = ppermute(found_now, "dp", pieces_in)
+        if s < y2 - w1:
+            x_new = ppermute(x_new, "dp", perm=so_far_all)
+            built = built + panel(x_new, (outcome_arr + s) % y2 * big)
+        block_next = panel(found_now, (outcome_arr - s) % y2 * big)
+        built = built + block_next
+    return built
 
 
 def feature_map(values):
@@ -35,11 +54,15 @@
     read = ask_state(query_feature, state / count, mass / count)
     mixed = finish_heads(read, count)
     mixed = mixed.reshape(mixed.shape[0], mixed.shape[1], -1)
-    return jnp.einsum(
-        "btw,wv->btv",
-        mixed,
-        lax.all_gather(out_weight, "dp", axis=0, tiled=True),
-        preferred_element_type=jnp.float32,
+    return _draft_counts(
+        out_weight,
+        0,
+        lambda own_block, start: jnp.einsum(
+            "btw,wv->btv",
+            lax.dynamic_slice_in_dim(mixed, start, own_block.shape[0], axis=2),
+            own_block,
+            preferred_element_type=jnp.float32,
+        ),
     ).astype(jnp.bfloat16)
 
 

time: 246 us -> 400 us (1.63)
  the two profiles are of different devices: /device:TPU:1 before, /device:TPU:128 now
where the time goes in v1:
time: 400 us
  waiting for transfers between devices  280 us (70%)
  starting transfers between devices  37.8 us (9%)
  matrix products  29.8 us (7%)
  blocking collectives  27.9 us (7%)
  between operations  13.7 us (3%)
  local copies, waits for them, and re-layouts  5.48 us (1%)
  other arithmetic  5.23 us (1%)
    ppermute x8, waiting for transfers between devices, _draft_counts(): found_now = ppermute(found_now, 'dp', pieces_in)  210 us
    ppermute x7, waiting for transfers between devices, _draft_counts(): x_new = ppermute(x_new, 'dp', perm=so_far_all)  69.9 us
    ppermute x7, starting transfers between devices, _draft_counts(): x_new = ppermute(x_new, 'dp', perm=so_far_all)  36.2 us
    psum x1, blocking collectives, body(): state, mass = lax.psum((part_state, part_mass), 'sp')  27.9 us
    dot_general x16, matrix products, body(): jnp.einsum('btw,wv->btv', lax.dynamic_slice_in_dim(mixed, start, own_bloc...  23.3 us
  transfers between devices with their start and end apart: 16, of which 11 were waited for; matrix products, arithmetic and copies ran while one was open for 9% of the time, Pallas kernels for 0%

profile of v1, /device:TPU:128, one launch (start us, length us, event | category | flops | bytes accessed | tf_op | source)
XLA Modules:
  0.0 399.5 jit_solution(12538098169008944301)
XLA Ops:
  6.5 0.0 copy-start
  6.5 0.0 all-reduce.2.cloned.1.call-start
  6.5 1.5 collective-permute-start.1
  8.0 3.9 collective-permute-start
  11.9 45.7 %collective-permute-done.1 = bf16[256,4096]{1,0:T(8,128)(2,1)S(1)} collective-permute-done((bf16[256,4096]{1,0:T(8,128)(2,1)}, bf16[256,4096]{1,0:T(8,128)(2,1)S(1)}, u32[]{:S(2)}, u32[]{:S(2)}) %collective-permute-start.1) | collective-permute-done | bytes 2097184 | tf_op jit(solution)/shard_map/ppermute | solution.py:17
  57.6 0.0 collective-permute-start.3
  57.6 0.0 collective-permute-done
  57.6 0.0 copy-start.10
  57.6 5.3 %collective-permute-start.2 = (bf16[256,4096]{1,0:T(8,128)(2,1)S(1)}, bf16[256,4096]{1,0:T(8,128)(2,1)S(1)}, u32[]{:S(2)}, u32[]{:S(2)}) collective-permute-start(bf16[256,4096]{1,0:T(8,128)(2,1)S(1)} %collective-permute-done), channel_id=1, source_target_pairs={{0,240},{16,0},{32,16},{48,32},{64,48},{80,64},{96,80},{112,96},{1... | collective-permute-start | bytes 6291464 | tf_op jit(solution)/shard_map/ppermute | solution.py:19
  62.9 44.6 %collective-permute-done.3 = bf16[256,4096]{1,0:T(8,128)(2,1)S(1)} collective-permute-done((bf16[256,4096]{1,0:T(8,128)(2,1)S(1)}, bf16[256,4096]{1,0:T(8,128)(2,1)S(1)}, u32[]{:S(2)}, u32[]{:S(2)}) %collective-permute-start.3) | collective-permute-done | bytes 2097184 | tf_op jit(solution)/shard_map/ppermute | solution.py:17
  107.6 0.0 collective-permute-start.5
  107.6 0.0 collective-permute-done.2
  107.6 0.0 copy-start.8
  107.6 5.3 %collective-permute-start.4 = (bf16[256,4096]{1,0:T(8,128)(2,1)S(1)}, bf16[256,4096]{1,0:T(8,128)(2,1)}, u32[]{:S(2)}, u32[]{:S(2)}) collective-permute-start(bf16[256,4096]{1,0:T(8,128)(2,1)S(1)} %collective-permute-done.2), channel_id=1, source_target_pairs={{0,240},{16,0},{32,16},{48,32},{64,48},{80,64},{96,80},{112,96},{1... | collective-permute-start | bytes 6291464 | tf_op jit(solution)/shard_map/ppermute | solution.py:19
  112.9 43.9 %collective-permute-done.5 = bf16[256,4096]{1,0:T(8,128)(2,1)} collective-permute-done((bf16[256,4096]{1,0:T(8,128)(2,1)S(1)}, bf16[256,4096]{1,0:T(8,128)(2,1)}, u32[]{:S(2)}, u32[]{:S(2)}) %collective-permute-start.5) | collective-permute-done | bytes 2097184 | tf_op jit(solution)/shard_map/ppermute | solution.py:17
  156.8 0.0 copy-done.3
  156.8 0.1 collective-permute-start.7
  156.9 2.8 fusion.28
  159.7 0.0 copy-done.8
  159.7 0.0 collective-permute-done.4
  159.7 5.4 %collective-permute-start.6 = (bf16[256,4096]{1,0:T(8,128)(2,1)}, bf16[256,4096]{1,0:T(8,128)(2,1)}, u32[]{:S(2)}, u32[]{:S(2)}) collective-permute-start(bf16[256,4096]{1,0:T(8,128)(2,1)} %collective-permute-done.4), channel_id=1, source_target_pairs={{0,240},{16,0},{32,16},{48,32},{64,48},{80,64},{96,80},{112,96},{1... | collective-permute-start | bytes 6291464 | tf_op jit(solution)/shard_map/ppermute | solution.py:19
  165.1 3.1 fusion.20
  168.2 0.0 all-reduce.2.cloned.1.call-update
  168.3 37.2 %collective-permute-done.7 = bf16[256,4096]{1,0:T(8,128)(2,1)} collective-permute-done((bf16[256,4096]{1,0:T(8,128)(2,1)}, bf16[256,4096]{1,0:T(8,128)(2,1)}, u32[]{:S(2)}, u32[]{:S(2)}) %collective-permute-start.7) | collective-permute-done | bytes 2097184 | tf_op jit(solution)/shard_map/ppermute | solution.py:17
  205.5 0.0 collective-permute-start.9
  205.5 0.0 copy-done.5
  205.5 2.4 fusion.16
  207.9 3.0 copy.11
  211.0 27.9 %psum.15 = f32[1,32,128]{2,1,0:T(8,128)S(1)} all-reduce(f32[1,32,128]{2,1,0:T(8,128)S(1)} %bitcast.120), channel_id=1, replica_groups=mesh['dp'=16,'sp'=8,'shift'=2] {'sp'}, use_global_device_ids=true, to_apply=%region_2.3 | all-reduce | flops 4096 | bytes 32768 | tf_op jit(solution)/shard_map/psum | solution.py:53
  238.9 0.9 fusion.86
  239.8 0.0 collective-permute-done.6
  239.8 5.5 %collective-permute-start.8 = (bf16[256,4096]{1,0:T(8,128)(2,1)}, bf16[256,4096]{1,0:T(8,128)(2,1)}, u32[]{:S(2)}, u32[]{:S(2)}) collective-permute-start(bf16[256,4096]{1,0:T(8,128)(2,1)} %collective-permute-done.6), channel_id=1, source_target_pairs={{0,240},{16,0},{32,16},{48,32},{64,48},{80,64},{96,80},{112,96},{1... | collective-permute-start | bytes 6291464 | tf_op jit(solution)/shard_map/ppermute | solution.py:19
  245.3 2.5 fusion.15
  247.8 5.4 %collective-permute-done.9 = bf16[256,4096]{1,0:T(8,128)(2,1)} collective-permute-done((bf16[256,4096]{1,0:T(8,128)(2,1)}, bf16[256,4096]{1,0:T(8,128)(2,1)}, u32[]{:S(2)}, u32[]{:S(2)}) %collective-permute-start.9) | collective-permute-done | bytes 2097184 | tf_op jit(solution)/shard_map/ppermute | solution.py:17
  253.2 0.0 collective-permute-start.11
  253.2 0.7 fusion.50
  253.9 0.8 copy-done.11
  254.8 0.8 convolution_add_fusion.8
  255.6 0.8 copy-done.7
  256.4 0.7 convolution_add_fusion.7
  257.1 0.8 copy-done.4
  258.0 0.7 fusion.45
  258.7 27.0 %collective-permute-done.8 = bf16[256,4096]{1,0:T(8,128)(2,1)} collective-permute-done((bf16[256,4096]{1,0:T(8,128)(2,1)}, bf16[256,4096]{1,0:T(8,128)(2,1)}, u32[]{:S(2)}, u32[]{:S(2)}) %collective-permute-start.8) | collective-permute-done | bytes 2097184 | tf_op jit(solution)/shard_map/ppermute | solution.py:19
  285.7 5.4 %collective-permute-start.10 = (bf16[256,4096]{1,0:T(8,128)(2,1)}, bf16[256,4096]{1,0:T(8,128)(2,1)S(1)}, u32[]{:S(2)}, u32[]{:S(2)}) collective-permute-start(bf16[256,4096]{1,0:T(8,128)(2,1)} %collective-permute-done.8), channel_id=1, source_target_pairs={{0,240},{16,0},{32,16},{48,32},{64,48},{80,64},{96,80},{112,96},{1... | collective-permute-start | bytes 6291464 | tf_op jit(solution)/shard_map/ppermute | solution.py:19
  291.1 0.8 fusion.5
  291.9 8.1 %collective-permute-done.11 = bf16[256,4096]{1,0:T(8,128)(2,1)S(1)} collective-permute-done((bf16[256,4096]{1,0:T(8,128)(2,1)}, bf16[256,4096]{1,0:T(8,128)(2,1)S(1)}, u32[]{:S(2)}, u32[]{:S(2)}) %collective-permute-start.11) | collective-permute-done | bytes 2097184 | tf_op jit(solution)/shard_map/ppermute | solution.py:17
  300.0 0.0 collective-permute-start.13
  300.0 2.3 fusion.42
  302.3 2.5 fusion.4
  304.8 2.3 fusion.39
  307.1 2.5 fusion.3
  309.6 22.1 %collective-permute-done.10 = bf16[256,4096]{1,0:T(8,128)(2,1)S(1)} collective-permute-done((bf16[256,4096]{1,0:T(8,128)(2,1)}, bf16[256,4096]{1,0:T(8,128)(2,1)S(1)}, u32[]{:S(2)}, u32[]{:S(2)}) %collective-permute-start.10) | collective-permute-done | bytes 2097184 | tf_op jit(solution)/shard_map/ppermute | solution.py:19
  331.7 5.4 %collective-permute-start.12 = (bf16[256,4096]{1,0:T(8,128)(2,1)S(1)}, bf16[256,4096]{1,0:T(8,128)(2,1)S(1)}, u32[]{:S(2)}, u32[]{:S(2)}) collective-permute-start(bf16[256,4096]{1,0:T(8,128)(2,1)S(1)} %collective-permute-done.10), channel_id=1, source_target_pairs={{0,240},{16,0},{32,16},{48,32},{64,48},{80,64},{96,80},{112,96},{1... | collective-permute-start | bytes 6291464 | tf_op jit(solution)/shard_map/ppermute | solution.py:19
  337.1 2.3 fusion.36
  339.4 6.3 %collective-permute-done.13 = bf16[256,4096]{1,0:T(8,128)(2,1)S(1)} collective-permute-done((bf16[256,4096]{1,0:T(8,128)(2,1)S(1)}, bf16[256,4096]{1,0:T(8,128)(2,1)S(1)}, u32[]{:S(2)}, u32[]{:S(2)}) %collective-permute-start.13) | collective-permute-done | bytes 2097184 | tf_op jit(solution)/shard_map/ppermute | solution.py:17
  345.8 0.0 collective-permute-start.14
  345.8 2.5 fusion.2
  348.2 0.7 fusion.33
  349.0 0.8 fusion.1
  349.8 0.7 fusion.30
  350.5 20.8 %collective-permute-done.12 = bf16[256,4096]{1,0:T(8,128)(2,1)S(1)} collective-permute-done((bf16[256,4096]{1,0:T(8,128)(2,1)S(1)}, bf16[256,4096]{1,0:T(8,128)(2,1)S(1)}, u32[]{:S(2)}, u32[]{:S(2)}) %collective-permute-start.12) | collective-permute-done | bytes 2097184 | tf_op jit(solution)/shard_map/ppermute | solution.py:19
  371.3 0.8 fusion
  372.0 18.6 %collective-permute-done.14 = bf16[256,4096]{1,0:T(8,128)(2,1)S(1)} collective-permute-done((bf16[256,4096]{1,0:T(8,128)(2,1)S(1)}, bf16[256,4096]{1,0:T(8,128)(2,1)S(1)}, u32[]{:S(2)}, u32[]{:S(2)}) %collective-permute-start.14) | collective-permute-done | bytes 2097184 | tf_op jit(solution)/shard_map/ppermute | solution.py:17
  390.6 2.1 fusion.7
  (18 shorter events, 0.0 us)
Async XLA Ops:
  6.5 158.6 %copy-start = (bf16[1,256,32,128]{3,2,1,0:T(8,128)(2,1)S(1)}, bf16[1,256,32,128]{3,2,1,0:T(8,128)(2,1)}, u32[]{:S(2)}) copy-start(bf16[1,256,32,128]{3,2,1,0:T(8,128)(2,1)} %param.6) | copy-start | bytes 6291460
  6.5 238.8 %all-reduce.2.cloned.1.call-start = ((), (), s32[]{:S(2)}) async-start(), calls=%async_computation | async-start | bytes 4194304 | tf_op jit(solution)/shard_map/psum | solution.py:53
  6.5 51.0 %collective-permute-start.1 = (bf16[256,4096]{1,0:T(8,128)(2,1)}, bf16[256,4096]{1,0:T(8,128)(2,1)S(1)}, u32[]{:S(2)}, u32[]{:S(2)}) collective-permute-start(bf16[256,4096]{1,0:T(8,128)(2,1)} %param.7), channel_id=1, source_target_pairs={{0,16},{16,32},{32,48},{48,64},{64,80},{80,96},{96,112},{112,128},... | collective-permute-start | bytes 6291464 | tf_op jit(solution)/shard_map/ppermute | solution.py:17
  8.0 49.6 %collective-permute-start = (bf16[256,4096]{1,0:T(8,128)(2,1)}, bf16[256,4096]{1,0:T(8,128)(2,1)S(1)}, u32[]{:S(2)}, u32[]{:S(2)}) collective-permute-start(bf16[256,4096]{1,0:T(8,128)(2,1)} %param.7), channel_id=1, source_target_pairs={{0,240},{16,0},{32,16},{48,32},{64,48},{80,64},{96,80},{112,96},{1... | collective-permute-start | bytes 6291464 | tf_op jit(solution)/shard_map/ppermute | solution.py:19
  57.6 99.2 %copy-start.6 = (bf16[256,4096]{1,0:T(8,128)(2,1)}, bf16[256,4096]{1,0:T(8,128)(2,1)S(1)}, u32[]{:S(2)}) copy-start(bf16[256,4096]{1,0:T(8,128)(2,1)S(1)} %collective-permute-done.1) | copy-start | bytes 6291460
  57.6 50.0 %collective-permute-start.3 = (bf16[256,4096]{1,0:T(8,128)(2,1)S(1)}, bf16[256,4096]{1,0:T(8,128)(2,1)S(1)}, u32[]{:S(2)}, u32[]{:S(2)}) collective-permute-start(bf16[256,4096]{1,0:T(8,128)(2,1)S(1)} %collective-permute-done.1), channel_id=1, source_target_pairs={{0,16},{16,32},{32,48},{48,64},{64,80},{80,96},{96,112},{112,128},... | collective-permute-start | bytes 6291464 | tf_op jit(solution)/shard_map/ppermute | solution.py:17
  57.6 99.2 %copy-start.10 = (bf16[256,4096]{1,0:T(8,128)(2,1)}, bf16[256,4096]{1,0:T(8,128)(2,1)S(1)}, u32[]{:S(2)}) copy-start(bf16[256,4096]{1,0:T(8,128)(2,1)S(1)} %collective-permute-done) | copy-start | bytes 6291460
  57.6 50.0 %collective-permute-start.2 = (bf16[256,4096]{1,0:T(8,128)(2,1)S(1)}, bf16[256,4096]{1,0:T(8,128)(2,1)S(1)}, u32[]{:S(2)}, u32[]{:S(2)}) collective-permute-start(bf16[256,4096]{1,0:T(8,128)(2,1)S(1)} %collective-permute-done), channel_id=1, source_target_pairs={{0,240},{16,0},{32,16},{48,32},{64,48},{80,64},{96,80},{112,96},{1... | collective-permute-start | bytes 6291464 | tf_op jit(solution)/shard_map/ppermute | solution.py:19
  107.6 49.2 %copy-start.3 = (bf16[256,4096]{1,0:T(8,128)(2,1)}, bf16[256,4096]{1,0:T(8,128)(2,1)S(1)}, u32[]{:S(2)}) copy-start(bf16[256,4096]{1,0:T(8,128)(2,1)S(1)} %collective-permute-done.3) | copy-start | bytes 6291460
  107.6 49.2 %collective-permute-start.5 = (bf16[256,4096]{1,0:T(8,128)(2,1)S(1)}, bf16[256,4096]{1,0:T(8,128)(2,1)}, u32[]{:S(2)}, u32[]{:S(2)}) collective-permute-start(bf16[256,4096]{1,0:T(8,128)(2,1)S(1)} %collective-permute-done.3), channel_id=1, source_target_pairs={{0,16},{16,32},{32,48},{48,64},{64,80},{80,96},{96,112},{112,128},... | collective-permute-start | bytes 6291464 | tf_op jit(solution)/shard_map/ppermute | solution.py:17
  107.6 52.1 %copy-start.8 = (bf16[256,4096]{1,0:T(8,128)(2,1)}, bf16[256,4096]{1,0:T(8,128)(2,1)S(1)}, u32[]{:S(2)}) copy-start(bf16[256,4096]{1,0:T(8,128)(2,1)S(1)} %collective-permute-done.2) | copy-start | bytes 6291460
  107.6 52.1 %collective-permute-start.4 = (bf16[256,4096]{1,0:T(8,128)(2,1)S(1)}, bf16[256,4096]{1,0:T(8,128)(2,1)}, u32[]{:S(2)}, u32[]{:S(2)}) collective-permute-start(bf16[256,4096]{1,0:T(8,128)(2,1)S(1)} %collective-permute-done.2), channel_id=1, source_target_pairs={{0,240},{16,0},{32,16},{48,32},{64,48},{80,64},{96,80},{112,96},{1... | collective-permute-start | bytes 6291464 | tf_op jit(solution)/shard_map/ppermute | solution.py:19
  156.8 48.7 %collective-permute-start.7 = (bf16[256,4096]{1,0:T(8,128)(2,1)}, bf16[256,4096]{1,0:T(8,128)(2,1)}, u32[]{:S(2)}, u32[]{:S(2)}) collective-permute-start(bf16[256,4096]{1,0:T(8,128)(2,1)} %collective-permute-done.5), channel_id=1, source_target_pairs={{0,16},{16,32},{32,48},{48,64},{64,80},{80,96},{96,112},{112,128},... | collective-permute-start | bytes 6291464 | tf_op jit(solution)/shard_map/ppermute | solution.py:17
  159.7 80.1 %collective-permute-start.6 = (bf16[256,4096]{1,0:T(8,128)(2,1)}, bf16[256,4096]{1,0:T(8,128)(2,1)}, u32[]{:S(2)}, u32[]{:S(2)}) collective-permute-start(bf16[256,4096]{1,0:T(8,128)(2,1)} %collective-permute-done.4), channel_id=1, source_target_pairs={{0,240},{16,0},{32,16},{48,32},{64,48},{80,64},{96,80},{112,96},{1... | collective-permute-start | bytes 6291464 | tf_op jit(solution)/shard_map/ppermute | solution.py:19
  168.2 37.2 %copy-start.5 = (bf16[1,256,32,128]{3,2,1,0:T(8,128)(2,1)S(1)}, bf16[1,256,32,128]{3,2,1,0:T(8,128)(2,1)}, u32[]{:S(2)}) copy-start(bf16[1,256,32,128]{3,2,1,0:T(8,128)(2,1)} %param.4) | copy-start | bytes 6291460
  205.5 47.7 %collective-permute-start.9 = (bf16[256,4096]{1,0:T(8,128)(2,1)}, bf16[256,4096]{1,0:T(8,128)(2,1)}, u32[]{:S(2)}, u32[]{:S(2)}) collective-permute-start(bf16[256,4096]{1,0:T(8,128)(2,1)} %collective-permute-done.7), channel_id=1, source_target_pairs={{0,16},{16,32},{32,48},{48,64},{64,80},{80,96},{96,112},{112,128},... | collective-permute-start | bytes 6291464 | tf_op jit(solution)/shard_map/ppermute | solution.py:17
  239.8 45.9 %collective-permute-start.8 = (bf16[256,4096]{1,0:T(8,128)(2,1)}, bf16[256,4096]{1,0:T(8,128)(2,1)}, u32[]{:S(2)}, u32[]{:S(2)}) collective-permute-start(bf16[256,4096]{1,0:T(8,128)(2,1)} %collective-permute-done.6), channel_id=1, source_target_pairs={{0,240},{16,0},{32,16},{48,32},{64,48},{80,64},{96,80},{112,96},{1... | collective-permute-start | bytes 6291464 | tf_op jit(solution)/shard_map/ppermute | solution.py:19
  245.3 7.9 %copy-start.2 = (bf16[256,4096]{1,0:T(8,128)(2,1)S(1)}, bf16[256,4096]{1,0:T(8,128)(2,1)}, u32[]{:S(2)}) copy-start(bf16[256,4096]{1,0:T(8,128)(2,1)} %param.7) | copy-start | bytes 6291460
  253.2 46.8 %collective-permute-start.11 = (bf16[256,4096]{1,0:T(8,128)(2,1)}, bf16[256,4096]{1,0:T(8,128)(2,1)S(1)}, u32[]{:S(2)}, u32[]{:S(2)}) collective-permute-start(bf16[256,4096]{1,0:T(8,128)(2,1)} %collective-permute-done.9), channel_id=1, source_target_pairs={{0,16},{16,32},{32,48},{48,64},{64,80},{80,96},{96,112},{112,128},... | collective-permute-start | bytes 6291464 | tf_op jit(solution)/shard_map/ppermute | solution.py:17
  253.2 1.6 copy-start.11
  254.8 1.6 copy-start.7
  256.4 1.6 copy-start.4
  258.0 33.1 %copy-start.9 = (bf16[256,4096]{1,0:T(8,128)(2,1)S(1)}, bf16[256,4096]{1,0:T(8,128)(2,1)}, u32[]{:S(2)}) copy-start(bf16[256,4096]{1,0:T(8,128)(2,1)} %copy-done.8) | copy-start | bytes 6291460
  285.7 46.0 %collective-permute-start.10 = (bf16[256,4096]{1,0:T(8,128)(2,1)}, bf16[256,4096]{1,0:T(8,128)(2,1)S(1)}, u32[]{:S(2)}, u32[]{:S(2)}) collective-permute-start(bf16[256,4096]{1,0:T(8,128)(2,1)} %collective-permute-done.8), channel_id=1, source_target_pairs={{0,240},{16,0},{32,16},{48,32},{64,48},{80,64},{96,80},{112,96},{1... | collective-permute-start | bytes 6291464 | tf_op jit(solution)/shard_map/ppermute | solution.py:19
  300.0 45.8 %collective-permute-start.13 = (bf16[256,4096]{1,0:T(8,128)(2,1)S(1)}, bf16[256,4096]{1,0:T(8,128)(2,1)S(1)}, u32[]{:S(2)}, u32[]{:S(2)}) collective-permute-start(bf16[256,4096]{1,0:T(8,128)(2,1)S(1)} %collective-permute-done.11), channel_id=1, source_target_pairs={{0,16},{16,32},{32,48},{48,64},{64,80},{80,96},{96,112},{112,128},... | collective-permute-start | bytes 6291464 | tf_op jit(solution)/shard_map/ppermute | solution.py:17
  331.7 39.5 %collective-permute-start.12 = (bf16[256,4096]{1,0:T(8,128)(2,1)S(1)}, bf16[256,4096]{1,0:T(8,128)(2,1)S(1)}, u32[]{:S(2)}, u32[]{:S(2)}) collective-permute-start(bf16[256,4096]{1,0:T(8,128)(2,1)S(1)} %collective-permute-done.10), channel_id=1, source_target_pairs={{0,240},{16,0},{32,16},{48,32},{64,48},{80,64},{96,80},{112,96},{1... | collective-permute-start | bytes 6291464 | tf_op jit(solution)/shard_map/ppermute | solution.py:19
  345.8 44.8 %collective-permute-start.14 = (bf16[256,4096]{1,0:T(8,128)(2,1)S(1)}, bf16[256,4096]{1,0:T(8,128)(2,1)S(1)}, u32[]{:S(2)}, u32[]{:S(2)}) collective-permute-start(bf16[256,4096]{1,0:T(8,128)(2,1)S(1)} %collective-permute-done.13), channel_id=1, source_target_pairs={{0,16},{16,32},{32,48},{48,64},{64,80},{80,96},{96,112},{112,128},... | collective-permute-start | bytes 6291464 | tf_op jit(solution)/shard_map/ppermute | solution.py:17
  390.6 2.1 copy-start.1
Sparse Core Ops, SparseCore 0:
  168.4 76.2 all-reduce.1
